TPU v7x, 32 devices: a whole 2x2x4 slice. The times are simulated.
32 devices in a mesh: row: 8 (over z, core), col: 4 (over y, x).
Axes of the slice: x: 2, y: 2, z: 4, core: 2. Of those that a mesh axis runs over, the one named last changes fastest.
Arguments:
- attn_out: bfloat16 [6, 512, 2048], P(None, 'col', 'row'), may hold values from -0.625 to 0.625
- out_cotangent: bfloat16 [6, 512, 2048], P(None, 'row', 'col'), may hold values from -6 to 6
- frozen: bfloat16 [6, 2048, 2048], P(None, 'row', 'col'), may hold values from -0.5 to 0.5
- adapt_in: bfloat16 [6, 32, 2048], P(None, None, 'row'), may hold values from -0.125 to 0.125
- adapt_out: bfloat16 [6, 32, 2048], P(None, None, 'col'), may hold values from -1 to 1
- magnitude: float32 [6, 2048], P(None, 'col'), may hold values from 0.1 to 1.9
Outputs:
- input_grad: bfloat16 [6, 512, 2048], P(None, 'col', 'row')
- adapt_in_grad: float32 [6, 32, 2048], P(None, None, 'row')
- adapt_out_grad: float32 [6, 32, 2048], P(None, None, 'col')
- magnitude_grad: float32 [6, 2048], P(None, 'col')
All inputs are finite; a program needn't handle non-finite values.
Results may differ from a plain program's by a relative error of at most 0.0065.
Values may be sent and summed in bfloat16 or wider, within the bound.
A program may use at most 64 MiB of HBM per device.

v0:
```python
import jax
import jax.numpy as jnp
from jax import lax
from jax.sharding import PartitionSpec as P

precise = lax.Precision.HIGHEST


def one_layer(acts, grads, frozen, adapt_in, adapt_out, magnitude):
    merged = frozen.astype(jnp.float32) + lax.dot_general(
        adapt_in, adapt_out, (((0,), (0,)), ((), ())), preferred_element_type=jnp.float32
    )
    squares_part = jnp.sum(merged * merged, axis=0)
    grads_all = lax.all_gather(grads, "row", axis=0, tiled=True)
    outer = lax.dot_general(
        lax.all_gather(acts, "col", axis=0, tiled=True),
        grads_all,
        (((0,), (0,)), ((), ())),
        preferred_element_type=jnp.float32,
    )
    dots_part = jnp.sum(merged * outer, axis=0)
    adapt_in_wide = adapt_in.astype(jnp.float32)
    inner_outer = jnp.dot(adapt_in_wide, outer, precision=precise)
    inner_merged = jnp.dot(adapt_in_wide, merged, precision=precise)
    squares, dots, inner_outer, inner_merged = lax.psum(
        (squares_part, dots_part, inner_outer, inner_merged), "row"
    )
    norms = jnp.sqrt(squares + 0.25)
    scales = magnitude / norms
    correct = -magnitude * dots / (norms * norms * norms)
    delta = outer * scales + merged * correct
    out_grad = inner_outer * scales + inner_merged * correct
    magnitude_grad = dots / norms
    in_part = lax.dot_general(
        adapt_out.astype(jnp.float32), delta, (((1,), (1,)), ((), ())), precision=precise
    )
    in_grad = lax.psum(in_part, "col")
    scaled = (grads_all * scales).astype(jnp.bfloat16)
    weight_low = merged.astype(jnp.bfloat16)
    summed = lax.psum_scatter(
        lax.dot_general(
            scaled, weight_low, (((1,), (1,)), ((), ())), preferred_element_type=jnp.float32
        ),
        "col",
        scatter_dimension=0,
        tiled=True,
    )
    return (summed.astype(jnp.bfloat16), in_grad, out_grad, magnitude_grad)


def body(attn_out, out_cotangent, frozen, adapt_in, adapt_out, magnitude):
    results = [
        one_layer(
            attn_out[layer_at],
            out_cotangent[layer_at],
            frozen[layer_at],
            adapt_in[layer_at],
            adapt_out[layer_at],
            magnitude[layer_at],
        )
        for layer_at in range(frozen.shape[0])
    ]
    return (
        jnp.stack([item[0] for item in results]),
        jnp.stack([item[1] for item in results]),
        jnp.stack([item[2] for item in results]),
        jnp.stack([item[3] for item in results]),
    )


def solution(mesh):
    return jax.shard_map(
        body,
        mesh=mesh,
        in_specs=(
            P(None, "col", "row"),
            P(None, "row", "col"),
            P(None, "row", "col"),
            P(None, None, "row"),
            P(None, None, "col"),
            P(None, "col"),
        ),
        out_specs=(
            P(None, "col", "row"),
            P(None, None, "row"),
            P(None, None, "col"),
            P(None, "col"),
        ),
        check_vma=False,
    )
```

profile of v0, /device:TPU:0, one launch (start us, length us, event | category | flops | bytes accessed | tf_op | source)
XLA Modules:
  0.0 473.6 jit_solution(1073232057520900545)
XLA Ops:
  7.2 1.1 fusion.151
  8.3 16.5 %all-gather = bf16[1,512,512]{2,1,0:T(8,128)(2,1)S(1)} all-gather(bf16[1,64,512]{2,1,0:T(8,128)(2,1)S(1)} %get-tuple-element.56), channel_id=2, replica_groups=mesh['row'=8,'col'=4] {'row'}, dimensions={1}, use_global_device_ids=true | all-gather | bytes 589824 | tf_op jit(solution)/shard_map/all_gather | solution.py:14
  24.8 9.0 %all-gather.6 = bf16[1,512,256]{2,1,0:T(8,128)(2,1)S(1)} all-gather(bf16[1,128,256]{2,1,0:T(8,128)(2,1)S(1)} %get-tuple-element.50), channel_id=8, replica_groups=mesh['row'=8,'col'=4] {'col'}, dimensions={1}, use_global_device_ids=true | all-gather | bytes 327680 | tf_op jit(solution)/shard_map/all_gather | solution.py:16
  33.8 15.0 %all-gather.1 = bf16[1,512,512]{2,1,0:T(8,128)(2,1)S(1)} all-gather(bf16[1,64,512]{2,1,0:T(8,128)(2,1)S(1)} %get-tuple-element.55), channel_id=3, replica_groups=mesh['row'=8,'col'=4] {'row'}, dimensions={1}, use_global_device_ids=true | all-gather | bytes 589824 | tf_op jit(solution)/shard_map/all_gather | solution.py:14
  48.8 9.1 %all-gather.7 = bf16[1,512,256]{2,1,0:T(8,128)(2,1)S(1)} all-gather(bf16[1,128,256]{2,1,0:T(8,128)(2,1)S(1)} %get-tuple-element.49), channel_id=9, replica_groups=mesh['row'=8,'col'=4] {'col'}, dimensions={1}, use_global_device_ids=true | all-gather | bytes 327680 | tf_op jit(solution)/shard_map/all_gather | solution.py:16
  59.2 14.9 %all-gather.2 = bf16[1,512,512]{2,1,0:T(8,128)(2,1)S(1)} all-gather(bf16[1,64,512]{2,1,0:T(8,128)(2,1)S(1)} %get-tuple-element.54), channel_id=4, replica_groups=mesh['row'=8,'col'=4] {'row'}, dimensions={1}, use_global_device_ids=true | all-gather | bytes 589824 | tf_op jit(solution)/shard_map/all_gather | solution.py:14
  74.1 8.0 %all-gather.8 = bf16[1,512,256]{2,1,0:T(8,128)(2,1)S(1)} all-gather(bf16[1,128,256]{2,1,0:T(8,128)(2,1)S(1)} %get-tuple-element.48), channel_id=10, replica_groups=mesh['row'=8,'col'=4] {'col'}, dimensions={1}, use_global_device_ids=true | all-gather | bytes 327680 | tf_op jit(solution)/shard_map/all_gather | solution.py:16
  82.7 15.0 %all-gather.3 = bf16[1,512,512]{2,1,0:T(8,128)(2,1)S(1)} all-gather(bf16[1,64,512]{2,1,0:T(8,128)(2,1)S(1)} %get-tuple-element.53), channel_id=5, replica_groups=mesh['row'=8,'col'=4] {'row'}, dimensions={1}, use_global_device_ids=true | all-gather | bytes 589824 | tf_op jit(solution)/shard_map/all_gather | solution.py:14
  97.7 8.9 %all-gather.9 = bf16[1,512,256]{2,1,0:T(8,128)(2,1)S(1)} all-gather(bf16[1,128,256]{2,1,0:T(8,128)(2,1)S(1)} %get-tuple-element.47), channel_id=11, replica_groups=mesh['row'=8,'col'=4] {'col'}, dimensions={1}, use_global_device_ids=true | all-gather | bytes 327680 | tf_op jit(solution)/shard_map/all_gather | solution.py:16
  107.3 14.8 %all-gather.4 = bf16[1,512,512]{2,1,0:T(8,128)(2,1)S(1)} all-gather(bf16[1,64,512]{2,1,0:T(8,128)(2,1)S(1)} %get-tuple-element.57), channel_id=6, replica_groups=mesh['row'=8,'col'=4] {'row'}, dimensions={1}, use_global_device_ids=true | all-gather | bytes 589824 | tf_op jit(solution)/shard_map/all_gather | solution.py:14
  122.1 8.1 %all-gather.10 = bf16[1,512,256]{2,1,0:T(8,128)(2,1)S(1)} all-gather(bf16[1,128,256]{2,1,0:T(8,128)(2,1)S(1)} %get-tuple-element.51), channel_id=12, replica_groups=mesh['row'=8,'col'=4] {'col'}, dimensions={1}, use_global_device_ids=true | all-gather | bytes 327680 | tf_op jit(solution)/shard_map/all_gather | solution.py:16
  130.8 15.0 %all-gather.5 = bf16[1,512,512]{2,1,0:T(8,128)(2,1)S(1)} all-gather(bf16[1,64,512]{2,1,0:T(8,128)(2,1)S(1)} %get-tuple-element.52), channel_id=7, replica_groups=mesh['row'=8,'col'=4] {'row'}, dimensions={1}, use_global_device_ids=true | all-gather | bytes 589824 | tf_op jit(solution)/shard_map/all_gather | solution.py:14
  145.8 9.1 %all-gather.11 = bf16[1,512,256]{2,1,0:T(8,128)(2,1)S(1)} all-gather(bf16[1,128,256]{2,1,0:T(8,128)(2,1)S(1)} %get-tuple-element.46), channel_id=13, replica_groups=mesh['row'=8,'col'=4] {'col'}, dimensions={1}, use_global_device_ids=true | all-gather | bytes 327680 | tf_op jit(solution)/shard_map/all_gather | solution.py:16
  156.4 27.6 %all-reduce = (f32[512]{0:T(512)}, f32[512]{0:T(512)}, f32[512]{0:T(512)S(1)}, f32[512]{0:T(512)S(1)}, f32[512]{0:T(512)S(1)}, /*index=5*/f32[512]{0:T(512)S(1)}...) all-reduce(f32[512]{0:T(512)S(1)} %get-tuple-element.15, ...), channel_id=1, replica_groups=mesh['row'=8,'col'=4] {'row'}, use_global_device_ids=true, to_apply=%region_1.0 | all-reduce | flops 6144 | bytes 49152 | tf_op jit(solution)/shard_map/psum | solution.py:25
  184.9 2.1 convolution_bitcast_fusion.17
  187.0 2.1 convolution_bitcast_fusion.16
  189.2 1.0 convolution_bitcast_fusion.15
  194.6 2.0 convolution_bitcast_fusion.11
  205.9 2.2 fusion
  208.2 2.2 fusion.1
  210.5 1.2 fusion.2
  211.8 1.1 fusion.3
  213.0 1.1 fusion.4
  214.2 1.1 fusion.5
  216.0 18.9 %all-reduce.8.cloned.1.call-done = (f32[1,32,256]{2,1,0:T(8,128)}, f32[1,32,256]{2,1,0:T(8,128)}, f32[1,32,256]{2,1,0:T(8,128)}, f32[1,32,256]{2,1,0:T(8,128)}, ...) async-done(((f32[1,32,256]{2,1,0:T(8,128)}, f32[1,32,256]{2,1,0:T(8,128)}, f32[1,32,256]{2,1,0:T(8,128)}, f32[1,32,256]{2,1,0:T(8,128)}, f32[1,32,256]{2,1,0:T(8,128)}, ...) | async-done | bytes 196624 | tf_op jit(solution)/shard_map/psum | solution.py:37
  239.5 59.2 %all-reduce.6.cloned.1.call-done = (f32[32,512]{1,0:T(8,128)}, f32[32,512]{1,0:T(8,128)}, f32[32,512]{1,0:T(8,128)}, f32[32,512]{1,0:T(8,128)}, f32[32,512]{1,0:...) async-done(((f32[32,512]{1,0:T(8,128)}, f32[32,512]{1,0:T(8,128)}, ...) | async-done | bytes 786448 | tf_op jit(solution)/shard_map/psum | solution.py:25
  304.1 21.6 %reduce-scatter.7.cloned.1.call-done = f32[128,256]{1,0:T(8,128)} async-done(((f32[512,256]{1,0:T(8,128)}), f32[128,256]{1,0:T(8,128)}) %reduce-scatter.7.cloned.1.call-update) | async-done | bytes 131088 | tf_op jit(solution)/shard_map/reduce_scatter | solution.py:40
  326.6 26.9 %reduce-scatter.9.cloned.1.call-done = f32[128,256]{1,0:T(8,128)} async-done(((f32[512,256]{1,0:T(8,128)}), f32[128,256]{1,0:T(8,128)}) %reduce-scatter.9.cloned.1.call-update) | async-done | bytes 131088 | tf_op jit(solution)/shard_map/reduce_scatter | solution.py:40
  354.5 26.9 %reduce-scatter.11.cloned.1.call-done = f32[128,256]{1,0:T(8,128)} async-done(((f32[512,256]{1,0:T(8,128)}), f32[128,256]{1,0:T(8,128)}) %reduce-scatter.11.cloned.1.call-update) | async-done | bytes 131088 | tf_op jit(solution)/shard_map/reduce_scatter | solution.py:40
  382.3 26.9 %reduce-scatter.13.cloned.1.call-done = f32[128,256]{1,0:T(8,128)} async-done(((f32[512,256]{1,0:T(8,128)}), f32[128,256]{1,0:T(8,128)}) %reduce-scatter.13.cloned.1.call-update) | async-done | bytes 131088 | tf_op jit(solution)/shard_map/reduce_scatter | solution.py:40
  410.1 27.0 %reduce-scatter.15.cloned.1.call-done = f32[128,256]{1,0:T(8,128)} async-done(((f32[512,256]{1,0:T(8,128)}), f32[128,256]{1,0:T(8,128)}) %reduce-scatter.15.cloned.1.call-update) | async-done | bytes 131088 | tf_op jit(solution)/shard_map/reduce_scatter | solution.py:40
  438.0 27.0 %reduce-scatter.17.cloned.1.call-done = f32[128,256]{1,0:T(8,128)} async-done(((f32[512,256]{1,0:T(8,128)}), f32[128,256]{1,0:T(8,128)}) %reduce-scatter.17.cloned.1.call-update) | async-done | bytes 131088 | tf_op jit(solution)/shard_map/reduce_scatter | solution.py:40
  (132 shorter events, 36.2 us)
Async XLA Ops:
  7.2 17.6 %copy-start.28 = (bf16[6,128,256]{2,1,0:T(8,128)(2,1)S(1)}, bf16[6,128,256]{2,1,0:T(8,128)(2,1)}, u32[]{:S(2)}) copy-start(bf16[6,128,256]{2,1,0:T(8,128)(2,1)} %param.6) | copy-start | bytes 1179652
  7.2 227.8 %all-reduce.8.cloned.1.call-start = ((), (), s32[]{:S(2)}) async-start(), calls=%async_computation.13 | async-start | bytes 393216 | tf_op jit(solution)/shard_map/psum | solution.py:37
  24.8 33.1 %copy-start.22 = (bf16[1,512,512]{2,1,0:T(8,128)(2,1)}, bf16[1,512,512]{2,1,0:T(8,128)(2,1)S(1)}, u32[]{:S(2)}) copy-start(bf16[1,512,512]{2,1,0:T(8,128)(2,1)S(1)} %all-gather) | copy-start | bytes 1572868
  48.8 10.1 %copy-start.19 = (bf16[1,512,512]{2,1,0:T(8,128)(2,1)}, bf16[1,512,512]{2,1,0:T(8,128)(2,1)S(1)}, u32[]{:S(2)}) copy-start(bf16[1,512,512]{2,1,0:T(8,128)(2,1)S(1)} %all-gather.1) | copy-start | bytes 1572868
  48.8 9.8 %copy-start.25 = (bf16[6,256,512]{2,1,0:T(8,128)(2,1)S(1)}, bf16[6,256,512]{2,1,0:T(8,128)(2,1)}, u32[]{:S(2)}) copy-start(bf16[6,256,512]{2,1,0:T(8,128)(2,1)} %param.8) | copy-start | bytes 4718596
  48.8 9.8 %copy-start.26 = (bf16[6,32,256]{2,1,0:T(8,128)(2,1)S(1)}, bf16[6,32,256]{2,1,0:T(8,128)(2,1)}, u32[]{:S(2)}) copy-start(bf16[6,32,256]{2,1,0:T(8,128)(2,1)} %param.9) | copy-start | bytes 294916
  48.8 9.8 %copy-start.27 = (bf16[6,32,512]{2,1,0:T(8,128)(2,1)S(1)}, bf16[6,32,512]{2,1,0:T(8,128)(2,1)}, u32[]{:S(2)}) copy-start(bf16[6,32,512]{2,1,0:T(8,128)(2,1)} %param.10) | copy-start | bytes 589828
  58.6 15.5 %copy-start = (f32[256,512]{1,0:T(8,128)}, f32[256,512]{1,0:T(8,128)S(1)}, u32[]{:S(2)}) copy-start(f32[256,512]{1,0:T(8,128)S(1)} %fusion.18) | copy-start | bytes 1572868
  74.1 8.6 %copy-start.23 = (bf16[1,512,512]{2,1,0:T(8,128)(2,1)}, bf16[1,512,512]{2,1,0:T(8,128)(2,1)S(1)}, u32[]{:S(2)}) copy-start(bf16[1,512,512]{2,1,0:T(8,128)(2,1)S(1)} %all-gather.2) | copy-start | bytes 1572868
  82.4 24.6 %copy-start.3 = (f32[256,512]{1,0:T(8,128)}, f32[256,512]{1,0:T(8,128)S(1)}, u32[]{:S(2)}) copy-start(f32[256,512]{1,0:T(8,128)S(1)} %fusion.15) | copy-start | bytes 1572868
  97.7 8.9 %copy-start.20 = (bf16[1,512,512]{2,1,0:T(8,128)(2,1)}, bf16[1,512,512]{2,1,0:T(8,128)(2,1)S(1)}, u32[]{:S(2)}) copy-start(bf16[1,512,512]{2,1,0:T(8,128)(2,1)S(1)} %all-gather.3) | copy-start | bytes 1572868
  107.0 23.2 %copy-start.6 = (f32[256,512]{1,0:T(8,128)}, f32[256,512]{1,0:T(8,128)S(1)}, u32[]{:S(2)}) copy-start(f32[256,512]{1,0:T(8,128)S(1)} %fusion.12) | copy-start | bytes 1572868
  122.1 23.7 %copy-start.17 = (bf16[1,512,512]{2,1,0:T(8,128)(2,1)}, bf16[1,512,512]{2,1,0:T(8,128)(2,1)S(1)}, u32[]{:S(2)}) copy-start(bf16[1,512,512]{2,1,0:T(8,128)(2,1)S(1)} %all-gather.4) | copy-start | bytes 1572868
  130.5 24.4 %copy-start.9 = (f32[256,512]{1,0:T(8,128)}, f32[256,512]{1,0:T(8,128)S(1)}, u32[]{:S(2)}) copy-start(f32[256,512]{1,0:T(8,128)S(1)} %fusion.9) | copy-start | bytes 1572868
  145.8 10.6 %copy-start.15 = (bf16[1,512,512]{2,1,0:T(8,128)(2,1)}, bf16[1,512,512]{2,1,0:T(8,128)(2,1)S(1)}, u32[]{:S(2)}) copy-start(bf16[1,512,512]{2,1,0:T(8,128)(2,1)S(1)} %all-gather.5) | copy-start | bytes 1572868
  145.8 10.6 %copy-start.31 = (f32[6,512]{1,0:T(8,128)S(1)}, f32[6,512]{1,0:T(8,128)}, u32[]{:S(2)}) copy-start(f32[6,512]{1,0:T(8,128)} %param.11) | copy-start | bytes 36868
  184.1 5.1 %copy-start.4 = (f32[256,512]{1,0:T(8,128)S(1)}, f32[256,512]{1,0:T(8,128)}, u32[]{:S(2)}) copy-start(f32[256,512]{1,0:T(8,128)} %copy-done.3) | copy-start | bytes 1572868
  184.9 5.4 %copy-start.7 = (f32[256,512]{1,0:T(8,128)S(1)}, f32[256,512]{1,0:T(8,128)}, u32[]{:S(2)}) copy-start(f32[256,512]{1,0:T(8,128)} %copy-done.6) | copy-start | bytes 1572868
  187.0 4.3 copy-start.10
  193.4 105.4 %all-reduce.6.cloned.1.call-start = ((), (), s32[]{:S(2)}) async-start(), calls=%async_computation.12 | async-start | bytes 1572864 | tf_op jit(solution)/shard_map/psum | solution.py:25
  193.7 5.7 %copy-start.5 = (f32[256,512]{1,0:T(8,128)S(1)}, f32[256,512]{1,0:T(8,128)}, u32[]{:S(2)}) copy-start(f32[256,512]{1,0:T(8,128)} %copy-done.3) | copy-start | bytes 1572868
  196.6 4.6 copy-start.8
  198.4 4.7 copy-start.11
  200.3 4.6 copy-start.14
  205.9 119.8 %reduce-scatter.7.cloned.1.call-start = ((), (), s32[]{:S(2)}) async-start(), calls=%async_computation.6 | async-start | bytes 655360 | tf_op jit(solution)/shard_map/reduce_scatter | solution.py:40
  208.2 145.4 %reduce-scatter.9.cloned.1.call-start = ((), (), s32[]{:S(2)}) async-start(), calls=%async_computation.7 | async-start | bytes 655360 | tf_op jit(solution)/shard_map/reduce_scatter | solution.py:40
  210.5 170.9 %reduce-scatter.11.cloned.1.call-start = ((), (), s32[]{:S(2)}) async-start(), calls=%async_computation.8 | async-start | bytes 655360 | tf_op jit(solution)/shard_map/reduce_scatter | solution.py:40
  211.7 197.4 %reduce-scatter.13.cloned.1.call-start = ((), (), s32[]{:S(2)}) async-start(), calls=%async_computation.9 | async-start | bytes 655360 | tf_op jit(solution)/shard_map/reduce_scatter | solution.py:40
  213.0 224.2 %reduce-scatter.15.cloned.1.call-start = ((), (), s32[]{:S(2)}) async-start(), calls=%async_computation.10 | async-start | bytes 655360 | tf_op jit(solution)/shard_map/reduce_scatter | solution.py:40
  214.2 250.9 %reduce-scatter.17.cloned.1.call-start = ((), (), s32[]{:S(2)}) async-start(), calls=%async_computation.11 | async-start | bytes 655360 | tf_op jit(solution)/shard_map/reduce_scatter | solution.py:40
  239.5 226.5 %copy-start.32 = (f32[6,32,256]{2,1,0:T(8,128)}, f32[6,32,256]{2,1,0:T(8,128)S(1)}, u32[]{:S(2)}) copy-start(f32[6,32,256]{2,1,0:T(8,128)S(1)} %constant_dynamic-update-slice_fusion) | copy-start | bytes 589828
  304.1 161.9 %copy-start.29 = (f32[6,32,512]{2,1,0:T(8,128)}, f32[6,32,512]{2,1,0:T(8,128)S(1)}, u32[]{:S(2)}) copy-start(f32[6,32,512]{2,1,0:T(8,128)S(1)} %bitcast_dynamic-update-slice_fusion) | copy-start | bytes 1179652
  (9 other events, 15.9 us)
Sparse Core Ops, SparseCore 0:
  193.5 41.3 all-reduce.7
  238.9 59.8 all-reduce.5
  301.6 24.0 reduce-scatter.6
  328.4 25.1 reduce-scatter.8
  356.2 25.0 reduce-scatter.10
  384.0 25.1 reduce-scatter.12
  412.0 25.0 reduce-scatter.14
  439.9 25.0 reduce-scatter.16
where the time goes:
time: 475 us; the launch traced here: 474 us
  waiting for transfers between devices  235 us (49%)
  blocking collectives  171 us (36%)
  matrix products  33.3 us (7%)
  between operations  14.5 us (3%)
  other arithmetic  11.6 us (2%)
  local copies, waits for them, and re-layouts  7.98 us (2%)
    reduce_scatter x6, waiting for transfers between devices, one_layer(): lax.psum_scatter(lax.dot_general(scaled, weight_low, (((1,), (1,)), ((),...  156 us
    all_gather x6, blocking collectives, one_layer(): grads_all = lax.all_gather(grads, 'row', axis=0, tiled=True)  91.1 us
    psum x1, waiting for transfers between devices, one_layer(): lax.psum((squares_part, dots_part, inner_outer, inner_merged), 'row')  59.2 us
    all_gather x6, blocking collectives, one_layer(): lax.all_gather(acts, 'col', axis=0, tiled=True)  52.2 us
    psum x1, blocking collectives, one_layer(): lax.psum((squares_part, dots_part, inner_outer, inner_merged), 'row')  27.6 us
    psum x1, waiting for transfers between devices, one_layer(): in_grad = lax.psum(in_part, 'col')  18.9 us
  transfers between devices with their start and end apart: 8, of which 8 were waited for; matrix products, arithmetic and copies ran while one was open for 8% of the time, Pallas kernels for 0%

commit v1 on v0

--- a/solution.py
+++ b/solution.py
@@ -11,7 +11,12 @@
         adapt_in, adapt_out, (((0,), (0,)), ((), ())), preferred_element_type=jnp.float32
     )
     squares_part = jnp.sum(merged * merged, axis=0)
-    grads_all = lax.all_gather(grads, "row", axis=0, tiled=True)
+    ring = [grads]
+    for hop in range(7):
+        ring.append(lax.ppermute(ring[-1], "row", [(dev, (dev + 1) % 8) for dev in range(8)]))
+    grads_all = jnp.roll(
+        jnp.concatenate(ring[::-1], axis=0), (lax.axis_index("row") + 1) * ring[0].shape[0], axis=0
+    )
     outer = lax.dot_general(
         lax.all_gather(acts, "col", axis=0, tiled=True),
         grads_all,

time: 475 us -> 440 us (0.926)
  blocking collectives: 171 us -> 80.3 us
  waiting for transfers between devices: 235 us -> 272 us
  starting transfers between devices: 0.51 us -> 13.1 us
    all_gather x6 -> x0, blocking collectives: 91.1 us -> none  [one_layer(): grads_all = lax.all_gather(grads, 'row', axis=0, tiled=True)]
    ppermute x0 -> x42, waiting for transfers between devices: none -> 28.3 us  [one_layer(): lax.ppermute(ring[-1], 'row', [(dev, (dev + 1) % 8) for dev in range(8)])]
    ppermute x0 -> x42, starting transfers between devices: none -> 12.8 us  [one_layer(): lax.ppermute(ring[-1], 'row', [(dev, (dev + 1) % 8) for dev in range(8)])]
    psum x1, waiting for transfers between devices: 18.9 us -> 28.1 us  [one_layer(): in_grad = lax.psum(in_part, 'col')]
  transfers between devices with their start and end apart: 8 -> 50, of which waited for: 8 -> 35; matrix products, arithmetic and copies ran while one was open for 8% -> 7% of each run, Pallas kernels for 0% -> 0%
where the time goes in v1:
time: 440 us; the launch traced here: 439 us
  waiting for transfers between devices  272 us (62%)
  blocking collectives  80.3 us (18%)
  matrix products  36.9 us (8%)
  between operations  14.9 us (3%)
  starting transfers between devices  13.1 us (3%)
  other arithmetic  11.6 us (3%)
  local copies, waits for them, and re-layouts  9.79 us (2%)
    reduce_scatter x6, waiting for transfers between devices, one_layer(): lax.psum_scatter(lax.dot_general(scaled, weight_low, (((1,), (1,)), ((),...  156 us
    psum x1, waiting for transfers between devices, one_layer(): lax.psum((squares_part, dots_part, inner_outer, inner_merged), 'row')  59.2 us
    all_gather x6, blocking collectives, one_layer(): lax.all_gather(acts, 'col', axis=0, tiled=True)  53.7 us
    ppermute x42, waiting for transfers between devices, one_layer(): lax.ppermute(ring[-1], 'row', [(dev, (dev + 1) % 8) for dev in range(8)])  28.3 us
    psum x1, waiting for transfers between devices, one_layer(): in_grad = lax.psum(in_part, 'col')  28.1 us
    psum x1, blocking collectives, one_layer(): lax.psum((squares_part, dots_part, inner_outer, inner_merged), 'row')  26.6 us
    ppermute x42, starting transfers between devices, one_layer(): lax.ppermute(ring[-1], 'row', [(dev, (dev + 1) % 8) for dev in range(8)])  12.8 us
    dot_general x6, matrix products, one_layer(): lax.dot_general(scaled, weight_low, (((1,), (1,)), ((), ())), preferred_e...  10.3 us
  transfers between devices with their start and end apart: 50, of which 35 were waited for; matrix products, arithmetic and copies ran while one was open for 7% of the time, Pallas kernels for 0%

profile of v1, /device:TPU:0, one launch (start us, length us, event | category | flops | bytes accessed | tf_op | source)
XLA Modules:
  0.0 438.8 jit_solution(14766243170486789337)
XLA Ops:
  8.8 2.7 collective-permute-start.28
  11.5 1.6 collective-permute-start.14
  13.2 1.5 collective-permute-done.35
  15.5 1.5 collective-permute-done.21
  18.7 1.6 collective-permute-done
  21.0 1.5 collective-permute-done.29
  24.1 1.6 collective-permute-done.8
  29.6 1.6 collective-permute-done.16
  35.1 1.6 collective-permute-done.24
  37.4 9.5 %all-gather = bf16[1,512,256]{2,1,0:T(8,128)(2,1)S(1)} all-gather(bf16[1,128,256]{2,1,0:T(8,128)(2,1)S(1)} %get-tuple-element.63), channel_id=2, replica_groups=mesh['row'=8,'col'=4] {'col'}, dimensions={1}, use_global_device_ids=true | all-gather | bytes 327680 | tf_op jit(solution)/shard_map/all_gather | solution.py:21
  46.9 9.0 %all-gather.1 = bf16[1,512,256]{2,1,0:T(8,128)(2,1)S(1)} all-gather(bf16[1,128,256]{2,1,0:T(8,128)(2,1)S(1)} %get-tuple-element.62), channel_id=3, replica_groups=mesh['row'=8,'col'=4] {'col'}, dimensions={1}, use_global_device_ids=true | all-gather | bytes 327680 | tf_op jit(solution)/shard_map/all_gather | solution.py:21
  56.5 1.7 collective-permute-start.40
  58.4 7.7 %all-gather.2 = bf16[1,512,256]{2,1,0:T(8,128)(2,1)S(1)} all-gather(bf16[1,128,256]{2,1,0:T(8,128)(2,1)S(1)} %get-tuple-element.61), channel_id=4, replica_groups=mesh['row'=8,'col'=4] {'col'}, dimensions={1}, use_global_device_ids=true | all-gather | bytes 327680 | tf_op jit(solution)/shard_map/all_gather | solution.py:21
  66.0 9.3 %all-gather.3 = bf16[1,512,256]{2,1,0:T(8,128)(2,1)S(1)} all-gather(bf16[1,128,256]{2,1,0:T(8,128)(2,1)S(1)} %get-tuple-element.60), channel_id=5, replica_groups=mesh['row'=8,'col'=4] {'col'}, dimensions={1}, use_global_device_ids=true | all-gather | bytes 327680 | tf_op jit(solution)/shard_map/all_gather | solution.py:21
  75.4 2.9 collective-permute-start.19
  78.6 9.4 %all-gather.4 = bf16[1,512,256]{2,1,0:T(8,128)(2,1)} all-gather(bf16[1,128,256]{2,1,0:T(8,128)(2,1)S(1)} %get-tuple-element.64), channel_id=6, replica_groups=mesh['row'=8,'col'=4] {'col'}, dimensions={1}, use_global_device_ids=true | all-gather | bytes 327680 | tf_op jit(solution)/shard_map/all_gather | solution.py:21
  87.9 9.0 %all-gather.5 = bf16[1,512,256]{2,1,0:T(8,128)(2,1)S(1)} all-gather(bf16[1,128,256]{2,1,0:T(8,128)(2,1)S(1)} %get-tuple-element.59), channel_id=7, replica_groups=mesh['row'=8,'col'=4] {'col'}, dimensions={1}, use_global_device_ids=true | all-gather | bytes 327680 | tf_op jit(solution)/shard_map/all_gather | solution.py:21
  99.1 3.4 collective-permute-done.34
  122.6 26.6 %all-reduce = (f32[512]{0:T(512)}, f32[512]{0:T(512)}, f32[512]{0:T(512)S(1)}, f32[512]{0:T(512)S(1)}, f32[512]{0:T(512)S(1)}, /*index=5*/f32[512]{0:T(512)S(1)}...) all-reduce(f32[512]{0:T(512)S(1)} %get-tuple-element.16, ...), channel_id=1, replica_groups=mesh['row'=8,'col'=4] {'row'}, use_global_device_ids=true, to_apply=%region_1.3 | all-reduce | flops 6144 | bytes 49152 | tf_op jit(solution)/shard_map/psum | solution.py:30
  150.0 2.2 convolution_bitcast_fusion.17
  152.2 2.1 convolution_bitcast_fusion.16
  158.7 2.0 convolution_bitcast_fusion.1
  160.7 2.3 fusion
  163.1 2.3 fusion.1
  172.1 28.1 %all-reduce.8.cloned.1.call-done = (f32[1,32,256]{2,1,0:T(8,128)}, f32[1,32,256]{2,1,0:T(8,128)}, f32[1,32,256]{2,1,0:T(8,128)}, f32[1,32,256]{2,1,0:T(8,128)}, ...) async-done(((f32[1,32,256]{2,1,0:T(8,128)}, f32[1,32,256]{2,1,0:T(8,128)}, f32[1,32,256]{2,1,0:T(8,128)}, f32[1,32,256]{2,1,0:T(8,128)}, f32[1,32,256]{2,1,0:T(8,128)}, ...) | async-done | bytes 196624 | tf_op jit(solution)/shard_map/psum | solution.py:42
  204.7 59.2 %all-reduce.6.cloned.1.call-done = (f32[32,512]{1,0:T(8,128)}, f32[32,512]{1,0:T(8,128)}, f32[32,512]{1,0:T(8,128)}, f32[32,512]{1,0:T(8,128)}, f32[32,512]{1,0:...) async-done(((f32[32,512]{1,0:T(8,128)}, f32[32,512]{1,0:T(8,128)}, ...) | async-done | bytes 786448 | tf_op jit(solution)/shard_map/psum | solution.py:30
  269.3 21.6 %reduce-scatter.7.cloned.1.call-done = f32[128,256]{1,0:T(8,128)} async-done(((f32[512,256]{1,0:T(8,128)}), f32[128,256]{1,0:T(8,128)}) %reduce-scatter.7.cloned.1.call-update) | async-done | bytes 131088 | tf_op jit(solution)/shard_map/reduce_scatter | solution.py:45
  291.9 26.9 %reduce-scatter.9.cloned.1.call-done = f32[128,256]{1,0:T(8,128)} async-done(((f32[512,256]{1,0:T(8,128)}), f32[128,256]{1,0:T(8,128)}) %reduce-scatter.9.cloned.1.call-update) | async-done | bytes 131088 | tf_op jit(solution)/shard_map/reduce_scatter | solution.py:45
  319.7 26.9 %reduce-scatter.11.cloned.1.call-done = f32[128,256]{1,0:T(8,128)} async-done(((f32[512,256]{1,0:T(8,128)}), f32[128,256]{1,0:T(8,128)}) %reduce-scatter.11.cloned.1.call-update) | async-done | bytes 131088 | tf_op jit(solution)/shard_map/reduce_scatter | solution.py:45
  347.5 26.9 %reduce-scatter.13.cloned.1.call-done = f32[128,256]{1,0:T(8,128)} async-done(((f32[512,256]{1,0:T(8,128)}), f32[128,256]{1,0:T(8,128)}) %reduce-scatter.13.cloned.1.call-update) | async-done | bytes 131088 | tf_op jit(solution)/shard_map/reduce_scatter | solution.py:45
  375.3 27.0 %reduce-scatter.15.cloned.1.call-done = f32[128,256]{1,0:T(8,128)} async-done(((f32[512,256]{1,0:T(8,128)}), f32[128,256]{1,0:T(8,128)}) %reduce-scatter.15.cloned.1.call-update) | async-done | bytes 131088 | tf_op jit(solution)/shard_map/reduce_scatter | solution.py:45
  403.2 27.0 %reduce-scatter.17.cloned.1.call-done = f32[128,256]{1,0:T(8,128)} async-done(((f32[512,256]{1,0:T(8,128)}), f32[128,256]{1,0:T(8,128)}) %reduce-scatter.17.cloned.1.call-update) | async-done | bytes 131088 | tf_op jit(solution)/shard_map/reduce_scatter | solution.py:45
  (249 shorter events, 65.6 us)
Async XLA Ops:
  7.2 193.0 %all-reduce.8.cloned.1.call-start = ((), (), s32[]{:S(2)}) async-start(), calls=%async_computation.13 | async-start | bytes 393216 | tf_op jit(solution)/shard_map/psum | solution.py:42
  8.3 6.5 %collective-permute-start.35 = (bf16[64,512]{1,0:T(8,128)(2,1)S(1)}, bf16[64,512]{1,0:T(8,128)(2,1)S(1)}, u32[]{:S(2)}, u32[]{:S(2)}) collective-permute-start(bf16[64,512]{1,0:T(8,128)(2,1)S(1)} %get-tuple-element.53), channel_id=1, source_target_pairs={{0,4},{4,8},{8,12},{12,16},{16,20},{20,24},{24,28},{28,0},{1,5},{5... | collective-permute-start | bytes 196616 | tf_op jit(solution)/shard_map/ppermute | solution.py:16
  8.8 6.7 %collective-permute-start.28 = (bf16[64,512]{1,0:T(8,128)(2,1)S(1)}, bf16[64,512]{1,0:T(8,128)(2,1)S(1)}, u32[]{:S(2)}, u32[]{:S(2)}) collective-permute-start(bf16[64,512]{1,0:T(8,128)(2,1)S(1)} %get-tuple-element.58), channel_id=1, source_target_pairs={{0,4},{4,8},{8,12},{12,16},{16,20},{20,24},{24,28},{28,0},{1,5},{5... | collective-permute-start | bytes 196616 | tf_op jit(solution)/shard_map/ppermute | solution.py:16
  11.5 6.1 %collective-permute-start.14 = (bf16[64,512]{1,0:T(8,128)(2,1)S(1)}, bf16[64,512]{1,0:T(8,128)(2,1)S(1)}, u32[]{:S(2)}, u32[]{:S(2)}) collective-permute-start(bf16[64,512]{1,0:T(8,128)(2,1)S(1)} %get-tuple-element.55), channel_id=1, source_target_pairs={{0,4},{4,8},{8,12},{12,16},{16,20},{20,24},{24,28},{28,0},{1,5},{5... | collective-permute-start | bytes 196616 | tf_op jit(solution)/shard_map/ppermute | solution.py:16
  15.5 5.5 %collective-permute-start.36 = (bf16[64,512]{1,0:T(8,128)(2,1)S(1)}, bf16[64,512]{1,0:T(8,128)(2,1)S(1)}, u32[]{:S(2)}, u32[]{:S(2)}) collective-permute-start(bf16[64,512]{1,0:T(8,128)(2,1)S(1)} %collective-permute-done.35), channel_id=1, source_target_pairs={{0,4},{4,8},{8,12},{12,16},{16,20},{20,24},{24,28},{28,0},{1,5},{5... | collective-permute-start | bytes 196616 | tf_op jit(solution)/shard_map/ppermute | solution.py:16
  33.4 22.4 %collective-permute-start.10 = (bf16[64,512]{1,0:T(8,128)(2,1)S(1)}, bf16[64,512]{1,0:T(8,128)(2,1)S(1)}, u32[]{:S(2)}, u32[]{:S(2)}) collective-permute-start(bf16[64,512]{1,0:T(8,128)(2,1)S(1)} %collective-permute-done.9), channel_id=1, source_target_pairs={{0,4},{4,8},{8,12},{12,16},{16,20},{20,24},{24,28},{28,0},{1,5},{5... | collective-permute-start | bytes 196616 | tf_op jit(solution)/shard_map/ppermute | solution.py:16
  34.1 21.8 %collective-permute-start.3 = (bf16[64,512]{1,0:T(8,128)(2,1)S(1)}, bf16[64,512]{1,0:T(8,128)(2,1)S(1)}, u32[]{:S(2)}, u32[]{:S(2)}) collective-permute-start(bf16[64,512]{1,0:T(8,128)(2,1)S(1)} %collective-permute-done.2), channel_id=1, source_target_pairs={{0,4},{4,8},{8,12},{12,16},{16,20},{20,24},{24,28},{28,0},{1,5},{5... | collective-permute-start | bytes 196616 | tf_op jit(solution)/shard_map/ppermute | solution.py:16
  35.1 21.3 %collective-permute-start.39 = (bf16[64,512]{1,0:T(8,128)(2,1)S(1)}, bf16[64,512]{1,0:T(8,128)(2,1)S(1)}, u32[]{:S(2)}, u32[]{:S(2)}) collective-permute-start(bf16[64,512]{1,0:T(8,128)(2,1)S(1)} %collective-permute-done.38), channel_id=1, source_target_pairs={{0,4},{4,8},{8,12},{12,16},{16,20},{20,24},{24,28},{28,0},{1,5},{5... | collective-permute-start | bytes 196616 | tf_op jit(solution)/shard_map/ppermute | solution.py:16
  36.7 19.8 %collective-permute-start.32 = (bf16[64,512]{1,0:T(8,128)(2,1)S(1)}, bf16[64,512]{1,0:T(8,128)(2,1)S(1)}, u32[]{:S(2)}, u32[]{:S(2)}) collective-permute-start(bf16[64,512]{1,0:T(8,128)(2,1)S(1)} %collective-permute-done.31), channel_id=1, source_target_pairs={{0,4},{4,8},{8,12},{12,16},{16,20},{20,24},{24,28},{28,0},{1,5},{5... | collective-permute-start | bytes 196616 | tf_op jit(solution)/shard_map/ppermute | solution.py:16
  37.4 20.9 %collective-permute-start.25 = (bf16[64,512]{1,0:T(8,128)(2,1)S(1)}, bf16[64,512]{1,0:T(8,128)(2,1)S(1)}, u32[]{:S(2)}, u32[]{:S(2)}) collective-permute-start(bf16[64,512]{1,0:T(8,128)(2,1)S(1)} %collective-permute-done.24), channel_id=1, source_target_pairs={{0,4},{4,8},{8,12},{12,16},{16,20},{20,24},{24,28},{28,0},{1,5},{5... | collective-permute-start | bytes 196616 | tf_op jit(solution)/shard_map/ppermute | solution.py:16
  55.9 19.4 %collective-permute-start.18 = (bf16[64,512]{1,0:T(8,128)(2,1)S(1)}, bf16[64,512]{1,0:T(8,128)(2,1)S(1)}, u32[]{:S(2)}, u32[]{:S(2)}) collective-permute-start(bf16[64,512]{1,0:T(8,128)(2,1)S(1)} %collective-permute-done.17), channel_id=1, source_target_pairs={{0,4},{4,8},{8,12},{12,16},{16,20},{20,24},{24,28},{28,0},{1,5},{5... | collective-permute-start | bytes 196616 | tf_op jit(solution)/shard_map/ppermute | solution.py:16
  55.9 19.4 %collective-permute-start.11 = (bf16[64,512]{1,0:T(8,128)(2,1)S(1)}, bf16[64,512]{1,0:T(8,128)(2,1)S(1)}, u32[]{:S(2)}, u32[]{:S(2)}) collective-permute-start(bf16[64,512]{1,0:T(8,128)(2,1)S(1)} %collective-permute-done.10), channel_id=1, source_target_pairs={{0,4},{4,8},{8,12},{12,16},{16,20},{20,24},{24,28},{28,0},{1,5},{5... | collective-permute-start | bytes 196616 | tf_op jit(solution)/shard_map/ppermute | solution.py:16
  56.5 21.9 %collective-permute-start.4 = (bf16[64,512]{1,0:T(8,128)(2,1)S(1)}, bf16[64,512]{1,0:T(8,128)(2,1)S(1)}, u32[]{:S(2)}, u32[]{:S(2)}) collective-permute-start(bf16[64,512]{1,0:T(8,128)(2,1)S(1)} %collective-permute-done.3), channel_id=1, source_target_pairs={{0,4},{4,8},{8,12},{12,16},{16,20},{20,24},{24,28},{28,0},{1,5},{5... | collective-permute-start | bytes 196616 | tf_op jit(solution)/shard_map/ppermute | solution.py:16
  56.5 21.9 %collective-permute-start.40 = (bf16[64,512]{1,0:T(8,128)(2,1)S(1)}, bf16[64,512]{1,0:T(8,128)(2,1)S(1)}, u32[]{:S(2)}, u32[]{:S(2)}) collective-permute-start(bf16[64,512]{1,0:T(8,128)(2,1)S(1)} %collective-permute-done.39), channel_id=1, source_target_pairs={{0,4},{4,8},{8,12},{12,16},{16,20},{20,24},{24,28},{28,0},{1,5},{5... | collective-permute-start | bytes 196616 | tf_op jit(solution)/shard_map/ppermute | solution.py:16
  58.3 20.2 %collective-permute-start.33 = (bf16[64,512]{1,0:T(8,128)(2,1)S(1)}, bf16[64,512]{1,0:T(8,128)(2,1)S(1)}, u32[]{:S(2)}, u32[]{:S(2)}) collective-permute-start(bf16[64,512]{1,0:T(8,128)(2,1)S(1)} %collective-permute-done.32), channel_id=1, source_target_pairs={{0,4},{4,8},{8,12},{12,16},{16,20},{20,24},{24,28},{28,0},{1,5},{5... | collective-permute-start | bytes 196616 | tf_op jit(solution)/shard_map/ppermute | solution.py:16
  75.3 21.6 %collective-permute-start.26 = (bf16[64,512]{1,0:T(8,128)(2,1)S(1)}, bf16[64,512]{1,0:T(8,128)(2,1)S(1)}, u32[]{:S(2)}, u32[]{:S(2)}) collective-permute-start(bf16[64,512]{1,0:T(8,128)(2,1)S(1)} %collective-permute-done.25), channel_id=1, source_target_pairs={{0,4},{4,8},{8,12},{12,16},{16,20},{20,24},{24,28},{28,0},{1,5},{5... | collective-permute-start | bytes 196616 | tf_op jit(solution)/shard_map/ppermute | solution.py:16
  75.4 21.6 %collective-permute-start.19 = (bf16[64,512]{1,0:T(8,128)(2,1)S(1)}, bf16[64,512]{1,0:T(8,128)(2,1)S(1)}, u32[]{:S(2)}, u32[]{:S(2)}) collective-permute-start(bf16[64,512]{1,0:T(8,128)(2,1)S(1)} %collective-permute-done.18), channel_id=1, source_target_pairs={{0,4},{4,8},{8,12},{12,16},{16,20},{20,24},{24,28},{28,0},{1,5},{5... | collective-permute-start | bytes 196616 | tf_op jit(solution)/shard_map/ppermute | solution.py:16
  78.3 19.3 %collective-permute-start.12 = (bf16[64,512]{1,0:T(8,128)(2,1)S(1)}, bf16[64,512]{1,0:T(8,128)(2,1)S(1)}, u32[]{:S(2)}, u32[]{:S(2)}) collective-permute-start(bf16[64,512]{1,0:T(8,128)(2,1)S(1)} %collective-permute-done.11), channel_id=1, source_target_pairs={{0,4},{4,8},{8,12},{12,16},{16,20},{20,24},{24,28},{28,0},{1,5},{5... | collective-permute-start | bytes 196616 | tf_op jit(solution)/shard_map/ppermute | solution.py:16
  78.4 19.3 %collective-permute-start.5 = (bf16[64,512]{1,0:T(8,128)(2,1)S(1)}, bf16[64,512]{1,0:T(8,128)(2,1)S(1)}, u32[]{:S(2)}, u32[]{:S(2)}) collective-permute-start(bf16[64,512]{1,0:T(8,128)(2,1)S(1)} %collective-permute-done.4), channel_id=1, source_target_pairs={{0,4},{4,8},{8,12},{12,16},{16,20},{20,24},{24,28},{28,0},{1,5},{5... | collective-permute-start | bytes 196616 | tf_op jit(solution)/shard_map/ppermute | solution.py:16
  78.5 20.2 %collective-permute-start.41 = (bf16[64,512]{1,0:T(8,128)(2,1)S(1)}, bf16[64,512]{1,0:T(8,128)(2,1)S(1)}, u32[]{:S(2)}, u32[]{:S(2)}) collective-permute-start(bf16[64,512]{1,0:T(8,128)(2,1)S(1)} %collective-permute-done.40), channel_id=1, source_target_pairs={{0,4},{4,8},{8,12},{12,16},{16,20},{20,24},{24,28},{28,0},{1,5},{5... | collective-permute-start | bytes 196616 | tf_op jit(solution)/shard_map/ppermute | solution.py:16
  96.9 5.5 %collective-permute-start.34 = (bf16[64,512]{1,0:T(8,128)(2,1)S(1)}, bf16[64,512]{1,0:T(8,128)(2,1)S(1)}, u32[]{:S(2)}, u32[]{:S(2)}) collective-permute-start(bf16[64,512]{1,0:T(8,128)(2,1)S(1)} %collective-permute-done.33), channel_id=1, source_target_pairs={{0,4},{4,8},{8,12},{12,16},{16,20},{20,24},{24,28},{28,0},{1,5},{5... | collective-permute-start | bytes 196616 | tf_op jit(solution)/shard_map/ppermute | solution.py:16
  97.0 6.2 %collective-permute-start.27 = (bf16[64,512]{1,0:T(8,128)(2,1)S(1)}, bf16[64,512]{1,0:T(8,128)(2,1)S(1)}, u32[]{:S(2)}, u32[]{:S(2)}) collective-permute-start(bf16[64,512]{1,0:T(8,128)(2,1)S(1)} %collective-permute-done.26), channel_id=1, source_target_pairs={{0,4},{4,8},{8,12},{12,16},{16,20},{20,24},{24,28},{28,0},{1,5},{5... | collective-permute-start | bytes 196616 | tf_op jit(solution)/shard_map/ppermute | solution.py:16
  97.6 6.2 %collective-permute-start.20 = (bf16[64,512]{1,0:T(8,128)(2,1)S(1)}, bf16[64,512]{1,0:T(8,128)(2,1)S(1)}, u32[]{:S(2)}, u32[]{:S(2)}) collective-permute-start(bf16[64,512]{1,0:T(8,128)(2,1)S(1)} %collective-permute-done.19), channel_id=1, source_target_pairs={{0,4},{4,8},{8,12},{12,16},{16,20},{20,24},{24,28},{28,0},{1,5},{5... | collective-permute-start | bytes 196616 | tf_op jit(solution)/shard_map/ppermute | solution.py:16
  97.7 6.9 %collective-permute-start.13 = (bf16[64,512]{1,0:T(8,128)(2,1)S(1)}, bf16[64,512]{1,0:T(8,128)(2,1)S(1)}, u32[]{:S(2)}, u32[]{:S(2)}) collective-permute-start(bf16[64,512]{1,0:T(8,128)(2,1)S(1)} %collective-permute-done.12), channel_id=1, source_target_pairs={{0,4},{4,8},{8,12},{12,16},{16,20},{20,24},{24,28},{28,0},{1,5},{5... | collective-permute-start | bytes 196616 | tf_op jit(solution)/shard_map/ppermute | solution.py:16
  98.7 6.5 %collective-permute-start.6 = (bf16[64,512]{1,0:T(8,128)(2,1)S(1)}, bf16[64,512]{1,0:T(8,128)(2,1)S(1)}, u32[]{:S(2)}, u32[]{:S(2)}) collective-permute-start(bf16[64,512]{1,0:T(8,128)(2,1)S(1)} %collective-permute-done.5), channel_id=1, source_target_pairs={{0,4},{4,8},{8,12},{12,16},{16,20},{20,24},{24,28},{28,0},{1,5},{5... | collective-permute-start | bytes 196616 | tf_op jit(solution)/shard_map/ppermute | solution.py:16
  158.6 105.4 %all-reduce.6.cloned.1.call-start = ((), (), s32[]{:S(2)}) async-start(), calls=%async_computation.12 | async-start | bytes 1572864 | tf_op jit(solution)/shard_map/psum | solution.py:30
  160.7 130.3 %reduce-scatter.7.cloned.1.call-start = ((), (), s32[]{:S(2)}) async-start(), calls=%async_computation.6 | async-start | bytes 655360 | tf_op jit(solution)/shard_map/reduce_scatter | solution.py:45
  163.1 155.7 %reduce-scatter.9.cloned.1.call-start = ((), (), s32[]{:S(2)}) async-start(), calls=%async_computation.7 | async-start | bytes 655360 | tf_op jit(solution)/shard_map/reduce_scatter | solution.py:45
  165.5 181.1 %reduce-scatter.11.cloned.1.call-start = ((), (), s32[]{:S(2)}) async-start(), calls=%async_computation.8 | async-start | bytes 655360 | tf_op jit(solution)/shard_map/reduce_scatter | solution.py:45
  167.0 207.4 %reduce-scatter.13.cloned.1.call-start = ((), (), s32[]{:S(2)}) async-start(), calls=%async_computation.9 | async-start | bytes 655360 | tf_op jit(solution)/shard_map/reduce_scatter | solution.py:45
  168.5 233.9 %reduce-scatter.15.cloned.1.call-start = ((), (), s32[]{:S(2)}) async-start(), calls=%async_computation.10 | async-start | bytes 655360 | tf_op jit(solution)/shard_map/reduce_scatter | solution.py:45
  170.0 260.3 %reduce-scatter.17.cloned.1.call-start = ((), (), s32[]{:S(2)}) async-start(), calls=%async_computation.11 | async-start | bytes 655360 | tf_op jit(solution)/shard_map/reduce_scatter | solution.py:45
  (49 other events, 659.4 us)
Sparse Core Ops, SparseCore 0:
  158.7 41.3 all-reduce.7
  204.1 59.8 all-reduce.5
  266.8 24.0 reduce-scatter.6
  293.6 25.1 reduce-scatter.8
  321.4 25.0 reduce-scatter.10
  349.2 25.1 reduce-scatter.12
  377.2 25.0 reduce-scatter.14
  405.2 25.0 reduce-scatter.16
